TPU v7x, 32 devices: a whole 2x2x4 slice. The times are simulated.
32 devices in a mesh: rows: 4 (over y, core), cols: 8 (over z, x).
Axes of the slice: x: 2, y: 2, z: 4, core: 2. Of those that a mesh axis runs over, the one named last changes fastest.
Arguments:
- terrain_grid: float32 [4096, 4096], P('rows', 'cols'), may hold values from -360 to 360
Outputs:
- shade: float32 [4096, 4096], P('rows', 'cols')
- first: float32 [2048, 2048], P('rows', 'cols')
- second: float32 [1024, 1024], P('rows', 'cols')
- third: float32 [512, 512], P('rows', 'cols')
All inputs are finite; a program needn't handle non-finite values.
Results may differ from a plain program's by a relative error of at most 0.0003.
Values sent between devices are 32-bit elements; how exact they have to be, the bound alone decides.
No kernel may reach another device: no remote copies, remote signals or barrier semaphores. Data moves between devices by JAX's collectives and lax.ppermute only.
A program may use at most 64 MiB of HBM per device.

v0:
```python
import math

import jax
import jax.numpy as jnp
from jax import lax
from jax.experimental import pallas as pl
from jax.experimental.pallas import tpu as pltpu
from jax.sharding import PartitionSpec as P

REACH = 120
HALO = 128
BORDER = 8
LANES = 128
BIG = float("inf")
light_up = math.sqrt(0.5)
VMEM = pl.BlockSpec(memory_space=pltpu.VMEM)
ANY = pl.BlockSpec(memory_space=pl.ANY)
HBM = pl.BlockSpec(memory_space=pltpu.HBM)
PICKS = ((jnp.maximum, -BIG), (jnp.minimum, BIG))


class Place:
    def __init__(self):
        row, col = lax.axis_index("rows"), lax.axis_index("cols")
        self.top, self.bottom = row == 0, row == lax.axis_size("rows") - 1
        self.left, self.right = col == 0, col == lax.axis_size("cols") - 1
        self.even_row, self.even_col = row % 2 == 0, col % 2 == 0


def down(t, shift, axis):
    return pltpu.roll(t, (-shift) % t.shape[axis], axis)


def multiple(i, size):
    return pl.multiple_of(i * size, size)


def fours(srcs, dsts, offset, rows, block):
    def step(i, carry):
        start = offset + multiple(i, block)
        both = [[src[pl.ds(start + tap, block), :] for tap in range(4)] for src in srcs]
        for (pick, _), (a, b, c, d), dst in zip(PICKS, both * (2 // len(srcs)), dsts):
            dst[pl.ds(start, block), :] = pick(pick(a, b), pick(c, d))
        return carry

    lax.fori_loop(0, rows // block, step, 0)


def tall_window(src, w4, put, pick, groups, first=0, last=1 << 20):
    levels = [{} for _ in range(5)]

    def join(a, b):
        return a if b is None else b if a is None else pick(a, b)

    def cells(g):
        return src[pl.ds(8 * g, 8), :] if first <= g < last else None

    def eight(g):
        return pick(w4[pl.ds(8 * g, 8), :], w4[pl.ds(8 * g + 4, 8), :]) if first - 1 <= g < last else None

    for g in range(groups + 29):
        levels[0][g] = eight(g)
        at = g
        for level, shift in enumerate((1, 2, 4, 8)):
            at -= shift
            if at >= 0:
                levels[level + 1][at] = join(levels[level].pop(at), levels[level][at + shift])
        out = g - 29
        if out >= 0:
            put(out, join(join(levels[4].pop(out), levels[4][out + 14]), cells(out + 30)))


def tent(in_lanes, out_lanes, in_size, place):
    shape = (in_lanes, out_lanes)
    col = lax.broadcasted_iota(jnp.int32, shape, 0)
    out = lax.broadcasted_iota(jnp.int32, shape, 1)
    out_size = in_size // 2
    col = jnp.where(col >= in_lanes - LANES // 2, col - in_lanes, col)
    out = jnp.where(out >= out_lanes - LANES // 2, out - out_lanes, out) if out_lanes > out_size else out
    low = jnp.where(place.left, 0, -in_lanes)
    out = jnp.maximum(out, low)
    out = jnp.minimum(out, jnp.where(place.right, out_size - 1, 2 * out_lanes))
    last = jnp.where(place.right, in_size - 1, 2 * in_lanes)
    total = jnp.zeros(shape, jnp.float32)
    for tap, weight in enumerate((0.125, 0.375, 0.375, 0.125)):
        spot = jnp.minimum(jnp.maximum(2 * out - 1 + tap, low), last)
        total = total + jnp.where(spot == col, weight, 0.0)
    return total.astype(jnp.bfloat16)


def fix_rows(ref, first, rows, place):
    @pl.when(place.top)
    def _():
        for tile in range(ref.shape[0]):
            ref[tile, pl.ds(first - 1, 1), :] = ref[tile, pl.ds(first, 1), :]

    @pl.when(place.bottom)
    def _():
        for tile in range(ref.shape[0]):
            ref[tile, pl.ds(first + rows, 1), :] = ref[tile, pl.ds(first + rows - 1, 1), :]


def slopes(p, west, east):
    return east - west, (east + west) + (p + p)


def shading(ab, lit, rows, block):
    count = ab.shape[0] // 2

    def step(i, carry):
        start = multiple(i, block)
        for tile in range(count):
            a = ab.at[2 * tile]
            b = ab.at[2 * tile + 1]
            north, here, south = (pl.ds(start + BORDER + shift, block) for shift in (-1, 0, 1))
            mid = a[here, :]
            gx = (a[north, :] + a[south, :]) + (mid + mid)
            gy = b[south, :] - b[north, :]
            lum = (light_up + 0.125 * (gx + gy)) * lax.rsqrt(1.0 + 0.0625 * (gx * gx + gy * gy))
            lit[tile, pl.ds(start, block), :] = jnp.maximum(lum, 0.0)
        return carry

    lax.fori_loop(0, rows // block, step, 0)


def halve_rows(src, dst, start, count):
    for tile in range(src.shape[0]):
        a, b, c, d = (src[tile, pl.ds(start + tap, count, stride=2), :] for tap in range(4))
        dst[tile, pl.ds(0, count), :] = ((a + d) + 3.0 * (b + c)) * 0.125


def row_levels(lit, u1, u2, u3, rows, place):
    fix_rows(lit, BORDER, rows, place)
    halve_rows(lit, u1, 1, rows // 2 + BORDER)
    fix_rows(u1, 3, rows // 2, place)
    halve_rows(u1, u2, 0, rows // 4 + BORDER)
    fix_rows(u2, 1, rows // 4, place)
    halve_rows(u2, u3, 0, rows // 8)


def lane_index(rows):
    return lax.broadcasted_iota(jnp.int32, (rows, LANES), 1)


def pack_kernel(x, a_ends, b_ends, a_mid, b_mid, to_y, to_core, sems):
    place = Place()
    rows, width = x.shape
    far = pl.multiple_of(width - LANES + 0 * lax.axis_index("cols"), LANES)
    a_lanes = pl.ds(pl.multiple_of(jnp.where(place.even_col, far, 0), LANES), LANES)
    b_lanes = pl.ds(pl.multiple_of(jnp.where(place.even_col, 0, far), LANES), LANES)
    low = rows - HALO
    y_rows = pl.ds(pl.multiple_of(jnp.where(place.even_row, 0, low), HALO), HALO)
    core_rows = pl.ds(pl.multiple_of(jnp.where(place.even_row, low, 0), HALO), HALO)
    pairs = []
    for lanes, ends, mid in ((b_lanes, b_ends, b_mid), (a_lanes, a_ends, a_mid)):
        pairs.append((x.at[pl.ds(0, HALO), lanes], ends.at[pl.ds(0, HALO), :]))
        pairs.append((x.at[pl.ds(low, HALO), lanes], ends.at[pl.ds(HALO, HALO), :]))
        pairs.append((x.at[pl.ds(HALO, low - HALO), lanes], mid))
    pairs.append((x.at[y_rows, :], to_y))
    pairs.append((x.at[core_rows, :], to_core))
    copies = [pltpu.make_async_copy(src, dst, sems.at[number]) for number, (src, dst) in enumerate(pairs)]
    for copy in copies:
        copy.start()
    for copy in copies:
        copy.wait()


def corner_kernel(a_ends, b_ends, to_y, to_core):
    even_row = Place().even_row
    y_rows = pl.ds(pl.multiple_of(jnp.where(even_row, 0, HALO), HALO), HALO)
    core_rows = pl.ds(pl.multiple_of(jnp.where(even_row, HALO, 0), HALO), HALO)
    for number, ends in enumerate((a_ends, b_ends)):
        lanes = pl.ds(number * LANES, LANES)
        to_y[:, lanes] = ends[y_rows, :]
        to_core[:, lanes] = ends[core_rows, :]


def halo_rows(dst, rows, by_core, by_y, first, last, place):
    below = HALO + rows

    @pl.when(jnp.logical_and(place.even_row, jnp.logical_not(place.top)))
    def _():
        dst(0, by_y)

    @pl.when(jnp.logical_not(place.even_row))
    def _():
        dst(0, by_core)

    @pl.when(jnp.logical_and(place.even_row, jnp.logical_not(place.bottom)))
    def _():
        dst(below, by_core)

    @pl.when(jnp.logical_and(jnp.logical_not(place.even_row), jnp.logical_not(place.bottom)))
    def _():
        dst(below, by_y)

    @pl.when(place.top)
    def _():
        dst(0, first)

    @pl.when(place.bottom)
    def _():
        dst(below, last)


def early_kernel(
    x, by_core, by_y,
    high, low, ends, beside, lit, u1, u2, u3, c1, c2, c3,
    xs, w_high, w_low, v_high, v_low, t_high, t_low, h_high, h_low, ab,
):
    place = Place()
    rows, width = x.shape
    tiles = width // LANES
    tall, deep = rows + 2 * BORDER, rows + 2 * HALO
    lanes_of = [slice(tile * LANES, (tile + 1) * LANES) for tile in range(tiles)]
    for tile in range(tiles):
        xs[tile, pl.ds(HALO, rows), :] = x[:, lanes_of[tile]]

    def whole_row(start, value):
        for tile in range(tiles):
            xs[tile, pl.ds(start, HALO), :] = jnp.broadcast_to(value[:, lanes_of[tile]], (HALO, LANES))

    halo_rows(whole_row, rows, by_core, by_y, x.at[pl.ds(0, 1), :], x.at[pl.ds(rows - 1, 1), :], place)

    def vertical(tile, carry):
        src = xs.at[tile]
        fours((src,), (w_high, w_low), 0, deep, 80)
        for (pick, _), w4, v in zip(PICKS, (w_high, w_low), (v_high, v_low)):

            def put(g, value, v=v):
                v[tile, pl.ds(8 * g, 8), :] = value

            tall_window(src, w4, put, pick, tall // 8)
        return carry

    lax.fori_loop(0, tiles, vertical, 0)

    for (_, spare), t, w in zip(PICKS, (t_high, t_low), (w_high, w_low)):
        for start in (0, HALO + width):
            t[pl.ds(start, HALO), :] = jnp.full((HALO, LANES), spare, jnp.float32)
        w[pl.ds(HALO + width, HALO), :] = jnp.full((HALO, LANES), spare, jnp.float32)

    def columns(i, carry):
        here = pl.ds(multiple(i, LANES), LANES)
        for v, t in ((v_high, t_high), (v_low, t_low)):
            for tile in range(tiles):
                t[pl.ds(HALO + tile * LANES, LANES), :] = v[tile, here, :].T
        fours((t_high, t_low), (w_high, w_low), REACH, width + BORDER, 104)
        for (pick, _), t, w4, h in zip(PICKS, (t_high, t_low), (w_high, w_low), (h_high, h_low)):

            def put(g, value, h=h):
                h[pl.ds(8 * g, 8), :] = value

            tall_window(t, w4, put, pick, (width + 2 * BORDER) // 8, HALO // 8, (HALO + width) // 8)
        own = pl.ds(multiple(i, LANES) + REACH, LANES)
        there = pl.ds(multiple(i, LANES) + BORDER, LANES)
        p = []
        for tile in range(tiles):
            at = pl.ds(BORDER + tile * LANES, LANES)
            mine = xs[tile, own, :]
            if tile in (0, tiles - 1):
                into = min(tile, 1)
                hi, lo = h_high[at, :].T, h_low[at, :].T
                high[into, here, :] = hi
                low[into, here, :] = lo
                ends[into, here, :] = mine
                p.append(mine - 0.5 * (hi + lo))
            else:
                p.append(mine - 0.5 * (h_high[at, :] + h_low[at, :]).T)
        for h, out in ((h_high, high), (h_low, low)):
            t = [h[pl.ds(width + BORDER, BORDER), :], h[pl.ds(2 * BORDER, LANES - 2 * BORDER), :], h[pl.ds(0, BORDER), :]]
            out[2, here, :] = jnp.concatenate(t, axis=0).T
        lane = lane_index(LANES)
        wests = [down(t, -1, 1) for t in p[:-1]]
        easts = [down(t, 1, 1) for t in p[1:]]
        for tile in range(1, tiles - 1):
            w = jnp.where(lane == 0, wests[tile - 1], wests[tile])
            e = jnp.where(lane == LANES - 1, easts[tile], easts[tile - 1])
            ab[2 * tile - 2, there, :], ab[2 * tile - 1, there, :] = slopes(p[tile], w, e)
        beside[here, :] = jnp.where(lane < LANES // 2, p[1], p[tiles - 2])
        return carry

    lax.fori_loop(0, pl.cdiv(tall, LANES), columns, 0)
    fix_rows(ab, 2 * BORDER, rows, place)
    shading(ab, lit, tall, 104)
    row_levels(lit, u1, u2, u3, rows, place)
    m1 = tent(width + LANES, width // 2 + LANES, width, place)
    m2 = tent(width // 2 + LANES, width // 4 + LANES, width // 2, place)
    m3 = tent(width // 4 + LANES, LANES, width // 4, place)
    c1[...] = m1[:, : width // 2]
    m12 = jnp.dot(m1, m2, preferred_element_type=jnp.float32).astype(jnp.bfloat16)
    c2[...] = m12[:, : width // 4]
    c3[...] = jnp.dot(m12, m3, preferred_element_type=jnp.float32).astype(jnp.bfloat16)


def two_pass(t, m):
    head = t.astype(jnp.bfloat16)
    tail = (t - head.astype(jnp.float32)).astype(jnp.bfloat16)
    return jnp.dot(head, m, preferred_element_type=jnp.float32) + jnp.dot(tail, m, preferred_element_type=jnp.float32)


def running(t, work, w4, pick, spare, sign):
    n = t.shape[0] // 8
    order = range(n - 1, -1, -1) if sign > 0 else range(n)
    total = None
    for g in order:
        part = t[8 * g : 8 * g + 8]
        total = part if total is None else pick(total, part)
        work[pl.ds(8 * g + 8, 8), :] = total
    work[pl.ds(8 * n + 8 if sign > 0 else 0, 8), :] = jnp.full((8, t.shape[1]), spare, jnp.float32)
    rows = 8 * n + 8 - 4
    base = 8 if sign > 0 else 1
    a, b, c, d = (work[pl.ds(base + tap, rows), :] for tap in range(4))
    w4[pl.ds(0, rows), :] = pick(pick(a, b), pick(c, d))
    return pick(w4[pl.ds(0, 8 * n), :], w4[pl.ds(4, 8 * n), :])


def late_kernel(
    a_ends, b_ends, a_mid, b_mid, by_core, by_y, high, low, ends, beside, lit_in, u1_in, u2_in, u3_in, c1, c2, c3,
    shade, first, second, third,
    strips, scans, work, w4s, w_high, w_low, walls, ab, lit, u1, u2, u3, f1, f2, f3, sems,
):
    place = Place()
    rows = a_mid.shape[0] + 2 * HALO
    tiles = lit_in.shape[0] + 2
    width = tiles * LANES
    tall, deep = rows + 2 * BORDER, rows + 2 * HALO
    copies = []

    def send(src, out, number):
        copies.append(pltpu.make_async_copy(src, out, sems.at[number]))
        copies[-1].start()

    def send_tile(src, tile):
        send(src.at[pl.ds(BORDER, rows), :], shade.at[:, pl.ds(tile * LANES, LANES)], tile)

    for tile in range(1, tiles - 1):
        send_tile(lit_in.at[tile - 1], tile)

    for kind, (tips, mid) in enumerate(((a_ends, a_mid), (b_ends, b_mid))):
        dst = strips.at[jnp.where(place.even_col, 1 - kind, kind)]
        lanes = pl.ds(kind * LANES, LANES)
        dst[pl.ds(HALO, HALO), :] = tips[pl.ds(0, HALO), :]
        dst[pl.ds(2 * HALO, rows - 2 * HALO), :] = mid[...]
        dst[pl.ds(rows, HALO), :] = tips[pl.ds(HALO, HALO), :]

        def write(start, value, dst=dst):
            dst[pl.ds(start, HALO), :] = jnp.broadcast_to(value[...], (HALO, LANES))

        edges = (tips.at[pl.ds(0, 1), :], tips.at[pl.ds(2 * HALO - 1, 1), :])
        halo_rows(write, rows, by_core.at[:, lanes], by_y.at[:, lanes], *edges, place)

    def scan(i, carry):
        here = pl.ds(multiple(i, LANES), LANES)
        for side, (sign, gone) in enumerate(((1, place.left), (-1, place.right))):
            t = strips[side, here, :].T
            for number, (pick, spare) in enumerate(PICKS):
                slot = 2 * side + number
                r = running(jnp.where(gone, spare, t), work.at[slot], w4s.at[slot], pick, spare, sign)
                r = jnp.concatenate([r[BORDER:], r[:BORDER]] if sign > 0 else [r[-BORDER:], r[:-BORDER]], axis=0)
                scans[slot, here, :] = r.T
        return carry

    lax.fori_loop(0, deep // LANES, scan, 0)

    def vertical(side, carry):
        srcs = (scans.at[2 * side], scans.at[2 * side + 1])
        fours(srcs, (w_high, w_low), 0, deep, 80)
        for number, (src, w4) in enumerate(zip(srcs, (w_high, w_low))):

            def put(g, value, number=number):
                walls[2 * side + number, pl.ds(8 * g, 8), :] = value

            tall_window(src, w4, put, PICKS[number][0], tall // 8)
        return carry

    lax.fori_loop(0, 2, vertical, 0)
    block = 104

    def combine(i, carry):
        start = multiple(i, block)
        here = pl.ds(start, block)
        there = pl.ds(start + BORDER, block)
        lane = lane_index(block)
        lh, ll, rh, rl = (walls[number, here, :] for number in range(4))
        body = lane < LANES - BORDER
        h = jnp.maximum(high[0, here, :], jnp.where(body, lh, -BIG))
        l = jnp.minimum(low[0, here, :], jnp.where(body, ll, BIG))
        near = ends[0, here, :] - 0.5 * (h + l)
        body = lane >= BORDER
        h = jnp.maximum(high[1, here, :], jnp.where(body, rh, -BIG))
        l = jnp.minimum(low[1, here, :], jnp.where(body, rl, BIG))
        far = ends[1, here, :] - 0.5 * (h + l)
        mine = lane < LANES // 2
        h = jnp.maximum(high[2, here, :], jnp.where(mine, rh, lh))
        l = jnp.minimum(low[2, here, :], jnp.where(mine, rl, ll))
        strip = pl.ds(start + REACH, block)
        spare = jnp.where(mine, strips[1, strip, :], strips[0, strip, :]) - 0.5 * (h + l)
        inner = beside[here, :]
        wests = [down(t, -1, 1) for t in (near, far, spare, inner)]
        easts = [down(t, 1, 1) for t in (near, far, spare, inner)]

        def west(tile, before):
            return jnp.where(lane == 0, before, wests[tile])

        def east(tile, after):
            return jnp.where(lane == LANES - 1, after, easts[tile])

        for tile, (p, w, e) in enumerate((
            (near, west(0, jnp.where(place.left, near, wests[2])), east(0, easts[3])),
            (far, west(1, wests[3]), east(1, jnp.where(place.right, far, easts[2]))),
            (spare, west(2, wests[1]), east(2, easts[0])),
        )):
            ab[2 * tile, there, :], ab[2 * tile + 1, there, :] = slopes(p, w, e)
        return carry

    lax.fori_loop(0, tall // block, combine, 0)
    fix_rows(ab, 2 * BORDER, rows, place)
    shading(ab, lit, tall, 104)
    send_tile(lit.at[0], 0)
    send_tile(lit.at[1], tiles - 1)
    row_levels(lit, u1, u2, u3, rows, place)

    def level(mine, inner, start, count, m):
        here = pl.ds(start, count)
        parts = [mine[0, here, :]] + [inner[tile, here, :] for tile in range(tiles - 2)] + [mine[1, here, :], mine[2, here, :]]
        return two_pass(jnp.concatenate(parts, axis=1), m[...])

    f1[...] = level(u1, u1_in, 3, rows // 2, c1)
    send(f1, first, tiles)
    f2[...] = level(u2, u2_in, 1, rows // 4, c2)
    send(f2, second, tiles + 1)
    f3[...] = level(u3, u3_in, 0, rows // 8, c3).T[: width // 8]
    send(f3, third, tiles + 2)
    for copy in copies:
        copy.wait()


def on_device(x):
    rows, width = x.shape
    f32, bf16 = jnp.float32, jnp.bfloat16
    tall, deep = rows + 2 * BORDER, rows + 2 * HALO
    most = pl.cdiv(tall, LANES) * LANES
    tiles = width // LANES
    shape = jax.ShapeDtypeStruct
    scratch = lambda *s: pltpu.VMEM(s, f32)

    def call(kernel, ins, outs, scratches, mib, flops, name):
        return pl.pallas_call(
            kernel,
            in_specs=ins,
            out_specs=[VMEM] * len(outs) if name != "late" else [ANY] * len(outs),
            out_shape=[shape(s, t) for s, t in outs],
            scratch_shapes=scratches,
            compiler_params=pltpu.CompilerParams(vmem_limit_bytes=mib * 2**20),
            cost_estimate=pl.CostEstimate(flops=flops, bytes_accessed=8_000_000, transcendentals=0),
        )

    def swap(value, axis, odd):
        count = lax.axis_size(axis)
        pairs = [(i, i + 1) for i in range(1 if odd else 0, count - 1, 2)]
        return lax.ppermute(value, axis, pairs + [(j, i) for i, j in pairs])

    tip, mid = ((2 * HALO, LANES), f32), ((rows - 2 * HALO, LANES), f32)
    edge, corner = ((HALO, width), f32), ((HALO, 2 * LANES), f32)
    sends = call(pack_kernel, [HBM], [tip, tip, mid, mid, edge, edge], [pltpu.SemaphoreType.DMA((8,))], 4, 1000, "pack")(x)
    b_ends = swap(sends[1], "cols", True)
    a_ends = swap(sends[0], "cols", False)
    b_mid = swap(sends[3], "cols", True)
    a_mid = swap(sends[2], "cols", False)
    by_y = swap(sends[4], "rows", True)
    by_core = swap(sends[5], "rows", False)
    to_y, to_core = call(corner_kernel, [VMEM, VMEM], [corner, corner], [], 2, 1000, "corner")(a_ends, b_ends)
    corner_y = swap(to_y, "rows", True)
    corner_core = swap(to_core, "rows", False)

    level_rows = (tall + BORDER, rows // 2 + 3 * BORDER, rows // 4 + 2 * BORDER, rows // 8)
    early = call(
        early_kernel,
        [VMEM] * 3,
        [
            ((3, most, LANES), f32),
            ((3, most, LANES), f32),
            ((2, most, LANES), f32),
            ((most, LANES), f32),
            *(((tiles - 2, n, LANES), f32) for n in level_rows),
            ((width + LANES, width // 2), bf16),
            ((width + LANES, width // 4), bf16),
            ((width + LANES, LANES), bf16),
        ],
        [
            scratch(tiles, deep + 8, LANES),
            scratch(deep + 8, LANES),
            scratch(deep + 8, LANES),
            scratch(tiles, most, LANES),
            scratch(tiles, most, LANES),
            scratch(width + 2 * HALO + 8, LANES),
            scratch(width + 2 * HALO + 8, LANES),
            scratch(width + 2 * BORDER, LANES),
            scratch(width + 2 * BORDER, LANES),
            scratch(2 * (tiles - 2), most + 2 * BORDER, LANES),
        ],
        20,
        80_000_000,
        "early",
    )(x, by_core, by_y)
    *outs, third = call(
        late_kernel,
        [VMEM] * 17,
        [((rows >> k, width >> k), f32) for k in range(3)] + [((width // 8, rows // 8), f32)],
        [
            scratch(2, deep + 8, LANES),
            scratch(4, deep + 8, LANES),
            scratch(4, LANES + 16, LANES),
            scratch(4, LANES + 8, LANES),
            scratch(deep + 8, LANES),
            scratch(deep + 8, LANES),
            scratch(4, tall, LANES),
            scratch(6, tall + 3 * BORDER, LANES),
            *(scratch(3, n, LANES) for n in level_rows),
            scratch(rows // 2, width // 2),
            scratch(rows // 4, width // 4),
            scratch(width // 8, rows // 8),
            pltpu.SemaphoreType.DMA((tiles + 3,)),
        ],
        20,
        80_000_000,
        "late",
    )(a_ends, b_ends, a_mid, b_mid, corner_core, corner_y, *early)
    return (*outs, third.T)


def solution(mesh):
    spec = P("rows", "cols")

    return jax.shard_map(on_device, mesh=mesh, in_specs=(spec,), out_specs=(spec,) * 4, check_vma=False)
```

profile of v0, /device:TPU:19, one launch (start us, length us, event | category | flops | bytes accessed | tf_op | source)
XLA Modules:
  0.0 45.1 jit_solution(10300120048849060584)
XLA Ops:
  0.6 0.0 copy-start
  0.6 1.6 %copy-done = f32[1024,512]{1,0:T(8,128)S(1)} copy-done((f32[1024,512]{1,0:T(8,128)S(1)}, f32[1024,512]{1,0:T(8,128)}, u32[]{:S(2)}) %copy-start) | copy-done | bytes 2097176
  2.2 0.0 copy-start.1
  2.2 0.3 shard_map.46
  2.5 0.3 collective-permute-start
  2.8 1.0 %collective-permute-start.6 = (f32[128,512]{1,0:T(8,128)S(1)}, f32[128,512]{1,0:T(8,128)S(1)}, u32[]{:S(2)}, u32[]{:S(2)}) collective-permute-start(f32[128,512]{1,0:T(8,128)S(1)} %get-tuple-element.33), channel_id=1, source_target_pairs={{0,8},{16,24},{8,0},{24,16},{1,9},{17,25},{9,1},{25,17},{2,10},{18... | collective-permute-start | bytes 786440 | tf_op jit(solution)/shard_map/ppermute | solution.py:462
  3.8 1.2 %collective-permute-start.2 = (f32[768,128]{1,0:T(8,128)S(1)}, f32[768,128]{1,0:T(8,128)S(1)}, u32[]{:S(2)}, u32[]{:S(2)}) collective-permute-start(f32[768,128]{1,0:T(8,128)S(1)} %get-tuple-element.29), channel_id=1, source_target_pairs={{0,1},{2,3},{4,5},{6,7},{1,0},{3,2},{5,4},{7,6},{8,9},{10,11},{12,... | collective-permute-start | bytes 1179656 | tf_op jit(solution)/shard_map/ppermute | solution.py:462
  5.0 3.2 %collective-permute-start.3 = (f32[768,128]{1,0:T(8,128)S(1)}, f32[768,128]{1,0:T(8,128)S(1)}, u32[]{:S(2)}, u32[]{:S(2)}) collective-permute-start(f32[768,128]{1,0:T(8,128)S(1)} %get-tuple-element.30), channel_id=1, source_target_pairs={{1,2},{3,4},{5,6},{2,1},{4,3},{6,5},{9,10},{11,12},{13,14},{10,9},... | collective-permute-start | bytes 1179656 | tf_op jit(solution)/shard_map/ppermute | solution.py:462
  8.2 3.6 %collective-permute-start.7 = (f32[128,512]{1,0:T(8,128)S(1)}, f32[128,512]{1,0:T(8,128)S(1)}, u32[]{:S(2)}, u32[]{:S(2)}) collective-permute-start(f32[128,512]{1,0:T(8,128)S(1)} %get-tuple-element.34), channel_id=1, source_target_pairs={{8,16},{16,8},{9,17},{17,9},{10,18},{18,10},{11,19},{19,11},{12,20... | collective-permute-start | bytes 786440 | tf_op jit(solution)/shard_map/ppermute | solution.py:462
  11.8 0.0 collective-permute-done.a_ends
  11.8 3.0 %collective-permute-start.1 = (f32[256,128]{1,0:T(8,128)S(1)}, f32[256,128]{1,0:T(8,128)S(1)}, u32[]{:S(2)}, u32[]{:S(2)}) collective-permute-start(f32[256,128]{1,0:T(8,128)S(1)} %get-tuple-element.28), channel_id=1, source_target_pairs={{1,2},{3,4},{5,6},{2,1},{4,3},{6,5},{9,10},{11,12},{13,14},{10,9},... | collective-permute-start | bytes 393224 | tf_op jit(solution)/shard_map/ppermute | solution.py:462
  14.8 6.2 %collective-permute-done.1.b_ends = f32[256,128]{1,0:T(8,128)S(1)} collective-permute-done((f32[256,128]{1,0:T(8,128)S(1)}, f32[256,128]{1,0:T(8,128)S(1)}, u32[]{:S(2)}, u32[]{:S(2)}) %collective-permute-start.1) | collective-permute-done | bytes 131104 | tf_op jit(solution)/shard_map/ppermute | solution.py:462
  21.0 1.3 %collective-permute-start.4 = (f32[128,256]{1,0:T(8,128)S(1)}, f32[128,256]{1,0:T(8,128)S(1)}, u32[]{:S(2)}, u32[]{:S(2)}) collective-permute-start(f32[128,256]{1,0:T(8,128)S(1)} %get-tuple-element.31), channel_id=1, source_target_pairs={{0,8},{16,24},{8,0},{24,16},{1,9},{17,25},{9,1},{25,17},{2,10},{18... | collective-permute-start | bytes 393224 | tf_op jit(solution)/shard_map/ppermute | solution.py:462
  22.3 0.0 collective-permute-done.6.by_core
  22.3 3.1 %collective-permute-start.5 = (f32[128,256]{1,0:T(8,128)S(1)}, f32[128,256]{1,0:T(8,128)S(1)}, u32[]{:S(2)}, u32[]{:S(2)}) collective-permute-start(f32[128,256]{1,0:T(8,128)S(1)} %get-tuple-element.32), channel_id=1, source_target_pairs={{8,16},{16,8},{9,17},{17,9},{10,18},{18,10},{11,19},{19,11},{12,20... | collective-permute-start | bytes 393224 | tf_op jit(solution)/shard_map/ppermute | solution.py:462
  25.4 0.0 collective-permute-done.7.by_y
  25.4 0.0 copy-done.1
  25.4 10.6 %shard_map.48 = (f32[3,1152,128]{2,1,0:T(8,128)S(1)}, f32[3,1152,128]{2,1,0:T(8,128)S(1)}, f32[2,1152,128]{2,1,0:T(8,128)S(1)}, f32[1152,128]{1,0:T(8,128)S(1)},...) custom-call(f32[1024,512]{1,0:T(8,128)S(1)} %copy-done.1, ...), custom_call_target="tpu_custom_call" | custom-call | flops 80000000 | bytes 8000000 | tf_op jit(solution)/shard_map/pallas_call | solution.py:478
  36.0 0.0 collective-permute-done.4.by_core
  36.0 0.0 collective-permute-done.5.by_y
  36.0 0.0 collective-permute-done.2.a_mid
  36.0 0.0 collective-permute-done.3.b_mid
  36.0 9.1 %shard_map.49 = (f32[1024,512]{1,0:T(8,128)}, f32[512,256]{1,0:T(8,128)}, f32[256,128]{1,0:T(8,128)}, f32[64,128]{1,0:T(8,128)}) custom-call(f32[256,128]{1,0:T(8,128)S(1)} %collective-permute-done.a_ends, f32[256,128]{1,0:T(8,128)S(1)} %collective-permute-done.1.b_ends, f32[768,128]{1,0:T(8,128)S(1)} %collective-permute-done.2.a_mid, ...), custom_call_target="tpu_custom_call" | custom-call | flops 80000000 | bytes 8000000 | tf_op jit(solution)/shard_map/pallas_call | solution.py:507
  (1 shorter events, 0.0 us)
Async XLA Ops:
  0.6 1.6 %copy-start = (f32[1024,512]{1,0:T(8,128)S(1)}, f32[1024,512]{1,0:T(8,128)}, u32[]{:S(2)}) copy-start(f32[1024,512]{1,0:T(8,128)} %x.3) | copy-start | bytes 6291460
  2.2 23.1 %copy-start.1 = (f32[1024,512]{1,0:T(8,128)S(1)}, f32[1024,512]{1,0:T(8,128)}, u32[]{:S(2)}) copy-start(f32[1024,512]{1,0:T(8,128)} %x.3) | copy-start | bytes 6291460
  2.5 9.3 %collective-permute-start = (f32[256,128]{1,0:T(8,128)S(1)}, f32[256,128]{1,0:T(8,128)S(1)}, u32[]{:S(2)}, u32[]{:S(2)}) collective-permute-start(f32[256,128]{1,0:T(8,128)S(1)} %get-tuple-element.27), channel_id=1, source_target_pairs={{0,1},{2,3},{4,5},{6,7},{1,0},{3,2},{5,4},{7,6},{8,9},{10,11},{12,... | collective-permute-start | bytes 393224 | tf_op jit(solution)/shard_map/ppermute | solution.py:462
  2.8 19.5 %collective-permute-start.6 = (f32[128,512]{1,0:T(8,128)S(1)}, f32[128,512]{1,0:T(8,128)S(1)}, u32[]{:S(2)}, u32[]{:S(2)}) collective-permute-start(f32[128,512]{1,0:T(8,128)S(1)} %get-tuple-element.33), channel_id=1, source_target_pairs={{0,8},{16,24},{8,0},{24,16},{1,9},{17,25},{9,1},{25,17},{2,10},{18... | collective-permute-start | bytes 786440 | tf_op jit(solution)/shard_map/ppermute | solution.py:462
  3.8 32.2 %collective-permute-start.2 = (f32[768,128]{1,0:T(8,128)S(1)}, f32[768,128]{1,0:T(8,128)S(1)}, u32[]{:S(2)}, u32[]{:S(2)}) collective-permute-start(f32[768,128]{1,0:T(8,128)S(1)} %get-tuple-element.29), channel_id=1, source_target_pairs={{0,1},{2,3},{4,5},{6,7},{1,0},{3,2},{5,4},{7,6},{8,9},{10,11},{12,... | collective-permute-start | bytes 1179656 | tf_op jit(solution)/shard_map/ppermute | solution.py:462
  5.0 31.0 %collective-permute-start.3 = (f32[768,128]{1,0:T(8,128)S(1)}, f32[768,128]{1,0:T(8,128)S(1)}, u32[]{:S(2)}, u32[]{:S(2)}) collective-permute-start(f32[768,128]{1,0:T(8,128)S(1)} %get-tuple-element.30), channel_id=1, source_target_pairs={{1,2},{3,4},{5,6},{2,1},{4,3},{6,5},{9,10},{11,12},{13,14},{10,9},... | collective-permute-start | bytes 1179656 | tf_op jit(solution)/shard_map/ppermute | solution.py:462
  8.2 17.2 %collective-permute-start.7 = (f32[128,512]{1,0:T(8,128)S(1)}, f32[128,512]{1,0:T(8,128)S(1)}, u32[]{:S(2)}, u32[]{:S(2)}) collective-permute-start(f32[128,512]{1,0:T(8,128)S(1)} %get-tuple-element.34), channel_id=1, source_target_pairs={{8,16},{16,8},{9,17},{17,9},{10,18},{18,10},{11,19},{19,11},{12,20... | collective-permute-start | bytes 786440 | tf_op jit(solution)/shard_map/ppermute | solution.py:462
  11.8 9.2 %collective-permute-start.1 = (f32[256,128]{1,0:T(8,128)S(1)}, f32[256,128]{1,0:T(8,128)S(1)}, u32[]{:S(2)}, u32[]{:S(2)}) collective-permute-start(f32[256,128]{1,0:T(8,128)S(1)} %get-tuple-element.28), channel_id=1, source_target_pairs={{1,2},{3,4},{5,6},{2,1},{4,3},{6,5},{9,10},{11,12},{13,14},{10,9},... | collective-permute-start | bytes 393224 | tf_op jit(solution)/shard_map/ppermute | solution.py:462
  21.0 15.0 %collective-permute-start.4 = (f32[128,256]{1,0:T(8,128)S(1)}, f32[128,256]{1,0:T(8,128)S(1)}, u32[]{:S(2)}, u32[]{:S(2)}) collective-permute-start(f32[128,256]{1,0:T(8,128)S(1)} %get-tuple-element.31), channel_id=1, source_target_pairs={{0,8},{16,24},{8,0},{24,16},{1,9},{17,25},{9,1},{25,17},{2,10},{18... | collective-permute-start | bytes 393224 | tf_op jit(solution)/shard_map/ppermute | solution.py:462
  22.3 13.7 %collective-permute-start.5 = (f32[128,256]{1,0:T(8,128)S(1)}, f32[128,256]{1,0:T(8,128)S(1)}, u32[]{:S(2)}, u32[]{:S(2)}) collective-permute-start(f32[128,256]{1,0:T(8,128)S(1)} %get-tuple-element.32), channel_id=1, source_target_pairs={{8,16},{16,8},{9,17},{17,9},{10,18},{18,10},{11,19},{19,11},{12,20... | collective-permute-start | bytes 393224 | tf_op jit(solution)/shard_map/ppermute | solution.py:462
where the time goes:
time: 45.3 us; the launch traced here: 45.1 us
  Pallas kernels  20 us (44%)
  starting transfers between devices  16.6 us (37%)
  waiting for transfers between devices  6.24 us (14%)
  local copies, waits for them, and re-layouts  1.59 us (4%)
  between operations  0.75 us (2%)
    ppermute x8, starting transfers between devices, swap(): return lax.ppermute(value, axis, pairs + [(j, i) for i, j in pairs])  16.6 us
    pallas_call x1, Pallas kernels, on_device(): call(early_kernel, [VMEM] * 3, [((3, most, LANES), f32), ((3, most, LANES...  10.6 us
    pallas_call x1, Pallas kernels, on_device(): call(late_kernel, [VMEM] * 17, [((rows >> k, width >> k), f32) for k in r...  9.08 us
    ppermute x8, waiting for transfers between devices, swap(): return lax.ppermute(value, axis, pairs + [(j, i) for i, j in pairs])  6.24 us
    unnamed x4, local copies, waits for them, and re-layouts  1.59 us
  transfers between devices with their start and end apart: 8, of which 1 were waited for; matrix products, arithmetic and copies ran while one was open for 0% of the time, Pallas kernels for 24%

commit v1 on v0

--- a/solution.py
+++ b/solution.py
@@ -2,6 +2,7 @@
 
 import jax
 import jax.numpy as jnp
+import numpy as np
 from jax import lax
 from jax.experimental import pallas as pl
 from jax.experimental.pallas import tpu as pltpu
@@ -16,6 +17,7 @@
 VMEM = pl.BlockSpec(memory_space=pltpu.VMEM)
 ANY = pl.BlockSpec(memory_space=pl.ANY)
 HBM = pl.BlockSpec(memory_space=pltpu.HBM)
+SLOTS = 3
 PICKS = ((jnp.maximum, -BIG), (jnp.minimum, BIG))
 
 
@@ -35,15 +37,19 @@
     return pl.multiple_of(i * size, size)
 
 
-def fours(srcs, dsts, offset, rows, block):
+def fours(srcs, dsts, offset, rows, block, inline=False):
     def step(i, carry):
-        start = offset + multiple(i, block)
+        start = offset + (i * block if inline else multiple(i, block))
         both = [[src[pl.ds(start + tap, block), :] for tap in range(4)] for src in srcs]
         for (pick, _), (a, b, c, d), dst in zip(PICKS, both * (2 // len(srcs)), dsts):
             dst[pl.ds(start, block), :] = pick(pick(a, b), pick(c, d))
         return carry
 
-    lax.fori_loop(0, rows // block, step, 0)
+    if inline:
+        for i in range(rows // block):
+            step(i, 0)
+    else:
+        lax.fori_loop(0, rows // block, step, 0)
 
 
 def tall_window(src, w4, put, pick, groups, first=0, last=1 << 20):
@@ -70,22 +76,28 @@
             put(out, join(join(levels[4].pop(out), levels[4][out + 14]), cells(out + 30)))
 
 
-def tent(in_lanes, out_lanes, in_size, place):
-    shape = (in_lanes, out_lanes)
-    col = lax.broadcasted_iota(jnp.int32, shape, 0)
-    out = lax.broadcasted_iota(jnp.int32, shape, 1)
+def tent(in_lanes, out_lanes, in_size, left, right):
     out_size = in_size // 2
-    col = jnp.where(col >= in_lanes - LANES // 2, col - in_lanes, col)
-    out = jnp.where(out >= out_lanes - LANES // 2, out - out_lanes, out) if out_lanes > out_size else out
-    low = jnp.where(place.left, 0, -in_lanes)
-    out = jnp.maximum(out, low)
-    out = jnp.minimum(out, jnp.where(place.right, out_size - 1, 2 * out_lanes))
-    last = jnp.where(place.right, in_size - 1, 2 * in_lanes)
-    total = jnp.zeros(shape, jnp.float32)
-    for tap, weight in enumerate((0.125, 0.375, 0.375, 0.125)):
-        spot = jnp.minimum(jnp.maximum(2 * out - 1 + tap, low), last)
-        total = total + jnp.where(spot == col, weight, 0.0)
-    return total.astype(jnp.bfloat16)
+    m = np.zeros((in_lanes, out_lanes))
+    for lane in range(out_lanes):
+        out = lane if lane < out_lanes - LANES // 2 or out_lanes == LANES else lane - out_lanes
+        out = max(out, 0) if left else out
+        out = min(out, out_size - 1) if right else out
+        for tap, weight in enumerate((0.125, 0.375, 0.375, 0.125)):
+            col = 2 * out - 1 + tap
+            col = max(col, 0) if left else col
+            col = min(col, in_size - 1) if right else col
+            if -LANES // 2 <= col < in_lanes - LANES // 2:
+                m[col % in_lanes, lane] += weight
+    return m
+
+
+def tents(width, left, right):
+    m1 = tent(width + LANES, width // 2 + LANES, width, left, right)
+    m2 = m1 @ tent(width // 2 + LANES, width // 4 + LANES, width // 2, left, right)
+    m3 = m2 @ tent(width // 4 + LANES, LANES, width // 4, left, right)
+    parts = (m1[:, : width // 2], m2[:, : width // 4], m3)
+    return jnp.concatenate([jnp.asarray(part, jnp.bfloat16) for part in parts], axis=1)
 
 
 def fix_rows(ref, first, rows, place):
@@ -149,13 +161,14 @@
     a_lanes = pl.ds(pl.multiple_of(jnp.where(place.even_col, far, 0), LANES), LANES)
     b_lanes = pl.ds(pl.multiple_of(jnp.where(place.even_col, 0, far), LANES), LANES)
     low = rows - HALO
+    head = a_ends.shape[0] - HALO
     y_rows = pl.ds(pl.multiple_of(jnp.where(place.even_row, 0, low), HALO), HALO)
     core_rows = pl.ds(pl.multiple_of(jnp.where(place.even_row, low, 0), HALO), HALO)
     pairs = []
     for lanes, ends, mid in ((b_lanes, b_ends, b_mid), (a_lanes, a_ends, a_mid)):
-        pairs.append((x.at[pl.ds(0, HALO), lanes], ends.at[pl.ds(0, HALO), :]))
-        pairs.append((x.at[pl.ds(low, HALO), lanes], ends.at[pl.ds(HALO, HALO), :]))
-        pairs.append((x.at[pl.ds(HALO, low - HALO), lanes], mid))
+        pairs.append((x.at[pl.ds(0, head), lanes], ends.at[pl.ds(0, head), :]))
+        pairs.append((x.at[pl.ds(low, HALO), lanes], ends.at[pl.ds(head, HALO), :]))
+        pairs.append((x.at[pl.ds(head, low - head), lanes], mid))
     pairs.append((x.at[y_rows, :], to_y))
     pairs.append((x.at[core_rows, :], to_core))
     copies = [pltpu.make_async_copy(src, dst, sems.at[number]) for number, (src, dst) in enumerate(pairs)]
@@ -167,8 +180,9 @@
 
 def corner_kernel(a_ends, b_ends, to_y, to_core):
     even_row = Place().even_row
-    y_rows = pl.ds(pl.multiple_of(jnp.where(even_row, 0, HALO), HALO), HALO)
-    core_rows = pl.ds(pl.multiple_of(jnp.where(even_row, HALO, 0), HALO), HALO)
+    low = a_ends.shape[0] - HALO
+    y_rows = pl.ds(pl.multiple_of(jnp.where(even_row, 0, low), HALO), HALO)
+    core_rows = pl.ds(pl.multiple_of(jnp.where(even_row, low, 0), HALO), HALO)
     for number, ends in enumerate((a_ends, b_ends)):
         lanes = pl.ds(number * LANES, LANES)
         to_y[:, lanes] = ends[y_rows, :]
@@ -205,8 +219,8 @@
 
 def early_kernel(
     x, by_core, by_y,
-    high, low, ends, beside, lit, u1, u2, u3, c1, c2, c3,
-    xs, w_high, w_low, v_high, v_low, t_high, t_low, h_high, h_low, ab,
+    high, low, ends, beside, lit, u1, u2, u3,
+    xs, w_high, w_low, v_high, v_low, t_high, t_low, q_high, q_low, h_high, h_low, ab,
 ):
     place = Place()
     rows, width = x.shape
@@ -235,39 +249,42 @@
 
     lax.fori_loop(0, tiles, vertical, 0)
 
-    for (_, spare), t, w in zip(PICKS, (t_high, t_low), (w_high, w_low)):
-        for start in (0, HALO + width):
-            t[pl.ds(start, HALO), :] = jnp.full((HALO, LANES), spare, jnp.float32)
-        w[pl.ds(HALO + width, HALO), :] = jnp.full((HALO, LANES), spare, jnp.float32)
-
-    def columns(i, carry):
-        here = pl.ds(multiple(i, LANES), LANES)
-        for v, t in ((v_high, t_high), (v_low, t_low)):
+    for (_, spare), t, w in zip(PICKS, (t_high, t_low), (q_high, q_low)):
+        for slot in range(SLOTS):
+            for start in (0, HALO + width):
+                t[slot, pl.ds(start, HALO), :] = jnp.full((HALO, LANES), spare, jnp.float32)
+            w[slot, pl.ds(HALO + width, HALO), :] = jnp.full((HALO, LANES), spare, jnp.float32)
+
+    def block(number, slot):
+        at_row = multiple(number, LANES)
+        here = pl.ds(at_row, LANES)
+        ts, ws, hs = ([pair[0].at[slot], pair[1].at[slot]] for pair in ((t_high, t_low), (q_high, q_low), (h_high, h_low)))
+        for v, t in zip((v_high, v_low), ts):
             for tile in range(tiles):
                 t[pl.ds(HALO + tile * LANES, LANES), :] = v[tile, here, :].T
-        fours((t_high, t_low), (w_high, w_low), REACH, width + BORDER, 104)
-        for (pick, _), t, w4, h in zip(PICKS, (t_high, t_low), (w_high, w_low), (h_high, h_low)):
+        fours(ts, ws, REACH, width + BORDER, 104, inline=True)
+        for (pick, _), t, w4, h in zip(PICKS, ts, ws, hs):
 
             def put(g, value, h=h):
                 h[pl.ds(8 * g, 8), :] = value
 
             tall_window(t, w4, put, pick, (width + 2 * BORDER) // 8, HALO // 8, (HALO + width) // 8)
-        own = pl.ds(multiple(i, LANES) + REACH, LANES)
-        there = pl.ds(multiple(i, LANES) + BORDER, LANES)
+        own = pl.ds(at_row + REACH, LANES)
+        there = pl.ds(at_row + BORDER, LANES)
         p = []
         for tile in range(tiles):
             at = pl.ds(BORDER + tile * LANES, LANES)
             mine = xs[tile, own, :]
             if tile in (0, tiles - 1):
                 into = min(tile, 1)
-                hi, lo = h_high[at, :].T, h_low[at, :].T
+                hi, lo = (h[at, :].T for h in hs)
                 high[into, here, :] = hi
                 low[into, here, :] = lo
                 ends[into, here, :] = mine
                 p.append(mine - 0.5 * (hi + lo))
             else:
-                p.append(mine - 0.5 * (h_high[at, :] + h_low[at, :]).T)
-        for h, out in ((h_high, high), (h_low, low)):
+                p.append(mine - 0.5 * (hs[0][at, :] + hs[1][at, :]).T)
+        for h, out in zip(hs, (high, low)):
             t = [h[pl.ds(width + BORDER, BORDER), :], h[pl.ds(2 * BORDER, LANES - 2 * BORDER), :], h[pl.ds(0, BORDER), :]]
             out[2, here, :] = jnp.concatenate(t, axis=0).T
         lane = lane_index(LANES)
@@ -277,26 +294,33 @@
             w = jnp.where(lane == 0, wests[tile - 1], wests[tile])
             e = jnp.where(lane == LANES - 1, easts[tile], easts[tile - 1])
             ab[2 * tile - 2, there, :], ab[2 * tile - 1, there, :] = slopes(p[tile], w, e)
-        beside[here, :] = jnp.where(lane < LANES // 2, p[1], p[tiles - 2])
-        return carry
-
-    lax.fori_loop(0, pl.cdiv(tall, LANES), columns, 0)
+        beside[here, :] = jnp.where(lane < LANES // 2, wests[tiles - 2], easts[0])
+
+    def columns(i, carry):
+        for slot in range(SLOTS):
+            block(i * SLOTS + slot, slot)
+        return carry
+
+    blocks = pl.cdiv(tall, LANES)
+    lax.fori_loop(0, blocks // SLOTS, columns, 0)
+    for number in range(blocks // SLOTS * SLOTS, blocks):
+        block(number, 0)
     fix_rows(ab, 2 * BORDER, rows, place)
     shading(ab, lit, tall, 104)
     row_levels(lit, u1, u2, u3, rows, place)
-    m1 = tent(width + LANES, width // 2 + LANES, width, place)
-    m2 = tent(width // 2 + LANES, width // 4 + LANES, width // 2, place)
-    m3 = tent(width // 4 + LANES, LANES, width // 4, place)
-    c1[...] = m1[:, : width // 2]
-    m12 = jnp.dot(m1, m2, preferred_element_type=jnp.float32).astype(jnp.bfloat16)
-    c2[...] = m12[:, : width // 4]
-    c3[...] = jnp.dot(m12, m3, preferred_element_type=jnp.float32).astype(jnp.bfloat16)
+
+
+def level_parts(width):
+    a, b = width // 2, width // 2 + width // 4
+    return (3, slice(0, a)), (1, slice(a, b)), (0, slice(b, b + LANES))
 
 
 def two_pass(t, m):
+    rows = t.shape[0]
     head = t.astype(jnp.bfloat16)
     tail = (t - head.astype(jnp.float32)).astype(jnp.bfloat16)
-    return jnp.dot(head, m, preferred_element_type=jnp.float32) + jnp.dot(tail, m, preferred_element_type=jnp.float32)
+    both = jnp.dot(jnp.concatenate([head, tail], axis=0), m, preferred_element_type=jnp.float32)
+    return both[:rows] + both[rows:]
 
 
 def running(t, work, w4, pick, spare, sign):
@@ -315,13 +339,74 @@
     return pick(w4[pl.ds(0, 8 * n), :], w4[pl.ds(4, 8 * n), :])
 
 
-def late_kernel(
-    a_ends, b_ends, a_mid, b_mid, by_core, by_y, high, low, ends, beside, lit_in, u1_in, u2_in, u3_in, c1, c2, c3,
-    shade, first, second, third,
-    strips, scans, work, w4s, w_high, w_low, walls, ab, lit, u1, u2, u3, f1, f2, f3, sems,
+def scan_block(strips, scans, number, turn, work, w4s, place):
+    here = pl.ds(multiple(number, LANES), LANES)
+    for side, (sign, gone) in enumerate(((1, place.left), (-1, place.right))):
+        t = strips[side, here, :].T
+        for kind, (pick, spare) in enumerate(PICKS):
+            slot = 2 * side + kind
+            spot = 4 * turn + slot
+            r = running(jnp.where(gone, spare, t), work.at[spot], w4s.at[spot], pick, spare, sign)
+            r = jnp.concatenate([r[BORDER:], r[:BORDER]] if sign > 0 else [r[-BORDER:], r[:-BORDER]], axis=0)
+            scans[slot, here, :] = r.T
+
+
+def middle_kernel(
+    a_ends, b_ends, by_core, by_y, u1, u2, u3, weights, weights_left, weights_right,
+    strips, scans, c, g1, g2, g3, work, w4s,
 ):
     place = Place()
-    rows = a_mid.shape[0] + 2 * HALO
+    deep = strips.shape[1] - 8
+    rows = deep - 2 * HALO
+    tiles = u1.shape[0] + 2
+    width = tiles * LANES
+    head = a_ends.shape[0] - HALO
+    for kind, tips in enumerate((a_ends, b_ends)):
+        dst = strips.at[jnp.where(place.even_col, 1 - kind, kind)]
+        lanes = pl.ds(kind * LANES, LANES)
+        dst[pl.ds(HALO, head), :] = tips[pl.ds(0, head), :]
+        dst[pl.ds(rows, HALO), :] = tips[pl.ds(head, HALO), :]
+
+        def write(start, value, dst=dst):
+            dst[pl.ds(start, HALO), :] = jnp.broadcast_to(value[...], (HALO, LANES))
+
+        edges = (tips.at[pl.ds(0, 1), :], tips.at[pl.ds(head + HALO - 1, 1), :])
+        halo_rows(write, rows, by_core.at[:, lanes], by_y.at[:, lanes], *edges, place)
+    blocks, ahead = deep // LANES, head // LANES + 1
+
+    def step(i, carry):
+        first = 2 * i + jnp.where(i == ahead // 2, blocks - 2 - ahead, 0)
+        for turn in range(2):
+            scan_block(strips, scans, first + turn, turn, work, w4s, place)
+        return carry
+
+    lax.fori_loop(0, ahead // 2 + 1, step, 0)
+    c[...] = weights[...]
+    few = 2 * BORDER
+
+    @pl.when(place.left)
+    def _():
+        c[pl.ds(0, few), :] = weights_left[pl.ds(0, few), :]
+        c[pl.ds(width + LANES - few, few), :] = weights_left[pl.ds(few, few), :]
+
+    @pl.when(place.right)
+    def _():
+        c[pl.ds(width - few, 2 * few), :] = weights_right[...]
+
+    for u, g, (start, lanes) in zip((u1, u2, u3), (g1, g2, g3), level_parts(width)):
+        here = pl.ds(start, g.shape[0])
+        t = jnp.concatenate([u[tile, here, :] for tile in range(tiles - 2)], axis=1)
+        g[...] = two_pass(t, c[LANES : width - LANES, lanes])
+
+
+def late_kernel(
+    a_mid, b_mid, strips_in, scans_in, c, g1, g2, g3, high, low, ends, beside, lit_in,
+    strips, scans, shade, first, second, third,
+    work, w4s, w_high, w_low, walls, ab, lit, u1, u2, u3, f1, f2, f3, sems,
+):
+    place = Place()
+    rows = strips.shape[1] - 8 - 2 * HALO
+    head = rows - HALO - a_mid.shape[0]
     tiles = lit_in.shape[0] + 2
     width = tiles * LANES
     tall, deep = rows + 2 * BORDER, rows + 2 * HALO
@@ -336,32 +421,15 @@
 
     for tile in range(1, tiles - 1):
         send_tile(lit_in.at[tile - 1], tile)
-
-    for kind, (tips, mid) in enumerate(((a_ends, a_mid), (b_ends, b_mid))):
-        dst = strips.at[jnp.where(place.even_col, 1 - kind, kind)]
-        lanes = pl.ds(kind * LANES, LANES)
-        dst[pl.ds(HALO, HALO), :] = tips[pl.ds(0, HALO), :]
-        dst[pl.ds(2 * HALO, rows - 2 * HALO), :] = mid[...]
-        dst[pl.ds(rows, HALO), :] = tips[pl.ds(HALO, HALO), :]
-
-        def write(start, value, dst=dst):
-            dst[pl.ds(start, HALO), :] = jnp.broadcast_to(value[...], (HALO, LANES))
-
-        edges = (tips.at[pl.ds(0, 1), :], tips.at[pl.ds(2 * HALO - 1, 1), :])
-        halo_rows(write, rows, by_core.at[:, lanes], by_y.at[:, lanes], *edges, place)
+    for kind, mid in enumerate((a_mid, b_mid)):
+        strips.at[jnp.where(place.even_col, 1 - kind, kind)][pl.ds(HALO + head, mid.shape[0]), :] = mid[...]
 
     def scan(i, carry):
-        here = pl.ds(multiple(i, LANES), LANES)
-        for side, (sign, gone) in enumerate(((1, place.left), (-1, place.right))):
-            t = strips[side, here, :].T
-            for number, (pick, spare) in enumerate(PICKS):
-                slot = 2 * side + number
-                r = running(jnp.where(gone, spare, t), work.at[slot], w4s.at[slot], pick, spare, sign)
-                r = jnp.concatenate([r[BORDER:], r[:BORDER]] if sign > 0 else [r[-BORDER:], r[:-BORDER]], axis=0)
-                scans[slot, here, :] = r.T
-        return carry
-
-    lax.fori_loop(0, deep // LANES, scan, 0)
+        for turn in range(2):
+            scan_block(strips, scans, head // LANES + 1 + 2 * i + turn, turn, work, w4s, place)
+        return carry
+
+    lax.fori_loop(0, a_mid.shape[0] // LANES // 2, scan, 0)
 
     def vertical(side, carry):
         srcs = (scans.at[2 * side], scans.at[2 * side + 1])
@@ -375,7 +443,7 @@
         return carry
 
     lax.fori_loop(0, 2, vertical, 0)
-    block = 104
+    block = 208
 
     def combine(i, carry):
         start = multiple(i, block)
@@ -397,8 +465,8 @@
         strip = pl.ds(start + REACH, block)
         spare = jnp.where(mine, strips[1, strip, :], strips[0, strip, :]) - 0.5 * (h + l)
         inner = beside[here, :]
-        wests = [down(t, -1, 1) for t in (near, far, spare, inner)]
-        easts = [down(t, 1, 1) for t in (near, far, spare, inner)]
+        wests = [down(t, -1, 1) for t in (near, far, spare)]
+        easts = [down(t, 1, 1) for t in (near, far, spare)]
 
         def west(tile, before):
             return jnp.where(lane == 0, before, wests[tile])
@@ -407,8 +475,8 @@
             return jnp.where(lane == LANES - 1, after, easts[tile])
 
         for tile, (p, w, e) in enumerate((
-            (near, west(0, jnp.where(place.left, near, wests[2])), east(0, easts[3])),
-            (far, west(1, wests[3]), east(1, jnp.where(place.right, far, easts[2]))),
+            (near, west(0, jnp.where(place.left, near, wests[2])), east(0, inner)),
+            (far, west(1, inner), east(1, jnp.where(place.right, far, easts[2]))),
             (spare, west(2, wests[1]), east(2, easts[0])),
         )):
             ab[2 * tile, there, :], ab[2 * tile + 1, there, :] = slopes(p, w, e)
@@ -421,16 +489,17 @@
     send_tile(lit.at[1], tiles - 1)
     row_levels(lit, u1, u2, u3, rows, place)
 
-    def level(mine, inner, start, count, m):
-        here = pl.ds(start, count)
-        parts = [mine[0, here, :]] + [inner[tile, here, :] for tile in range(tiles - 2)] + [mine[1, here, :], mine[2, here, :]]
-        return two_pass(jnp.concatenate(parts, axis=1), m[...])
-
-    f1[...] = level(u1, u1_in, 3, rows // 2, c1)
+    def level(u, inner, number):
+        start, lanes = level_parts(width)[number]
+        t = jnp.concatenate([u[tile, pl.ds(start, inner.shape[0]), :] for tile in range(3)], axis=1)
+        m = jnp.concatenate([c[:LANES, lanes], c[width - LANES :, lanes]], axis=0)
+        return inner[...] + two_pass(t, m)
+
+    f1[...] = level(u1, g1, 0)
     send(f1, first, tiles)
-    f2[...] = level(u2, u2_in, 1, rows // 4, c2)
+    f2[...] = level(u2, g2, 1)
     send(f2, second, tiles + 1)
-    f3[...] = level(u3, u3_in, 0, rows // 8, c3).T[: width // 8]
+    f3[...] = level(u3, g3, 2).T[: width // 8]
     send(f3, third, tiles + 2)
     for copy in copies:
         copy.wait()
@@ -445,11 +514,12 @@
     shape = jax.ShapeDtypeStruct
     scratch = lambda *s: pltpu.VMEM(s, f32)
 
-    def call(kernel, ins, outs, scratches, mib, flops, name):
+    def call(kernel, ins, outs, scratches, mib, flops, spaces=None, aliases={}):
         return pl.pallas_call(
             kernel,
             in_specs=ins,
-            out_specs=[VMEM] * len(outs) if name != "late" else [ANY] * len(outs),
+            out_specs=spaces or [VMEM] * len(outs),
+            input_output_aliases=aliases,
             out_shape=[shape(s, t) for s, t in outs],
             scratch_shapes=scratches,
             compiler_params=pltpu.CompilerParams(vmem_limit_bytes=mib * 2**20),
@@ -463,17 +533,21 @@
 
     tip, mid = ((2 * HALO, LANES), f32), ((rows - 2 * HALO, LANES), f32)
     edge, corner = ((HALO, width), f32), ((HALO, 2 * LANES), f32)
-    sends = call(pack_kernel, [HBM], [tip, tip, mid, mid, edge, edge], [pltpu.SemaphoreType.DMA((8,))], 4, 1000, "pack")(x)
+    sends = call(pack_kernel, [HBM], [tip, tip, mid, mid, edge, edge], [pltpu.SemaphoreType.DMA((8,))], 4, 1000)(x)
     b_ends = swap(sends[1], "cols", True)
     a_ends = swap(sends[0], "cols", False)
     b_mid = swap(sends[3], "cols", True)
     a_mid = swap(sends[2], "cols", False)
     by_y = swap(sends[4], "rows", True)
     by_core = swap(sends[5], "rows", False)
-    to_y, to_core = call(corner_kernel, [VMEM, VMEM], [corner, corner], [], 2, 1000, "corner")(a_ends, b_ends)
+    to_y, to_core = call(corner_kernel, [VMEM, VMEM], [corner, corner], [], 2, 1000)(a_ends, b_ends)
     corner_y = swap(to_y, "rows", True)
     corner_core = swap(to_core, "rows", False)
 
+    few = 2 * BORDER
+    at_left, at_right = tents(width, True, False), tents(width, False, True)
+    at_left = jnp.concatenate([at_left[:few], at_left[width + LANES - few :]], axis=0)
+    at_right = at_right[width - few : width + few]
     level_rows = (tall + BORDER, rows // 2 + 3 * BORDER, rows // 4 + 2 * BORDER, rows // 8)
     early = call(
         early_kernel,
@@ -484,9 +558,6 @@
             ((2, most, LANES), f32),
             ((most, LANES), f32),
             *(((tiles - 2, n, LANES), f32) for n in level_rows),
-            ((width + LANES, width // 2), bf16),
-            ((width + LANES, width // 4), bf16),
-            ((width + LANES, LANES), bf16),
         ],
         [
             scratch(tiles, deep + 8, LANES),
@@ -494,25 +565,31 @@
             scratch(deep + 8, LANES),
             scratch(tiles, most, LANES),
             scratch(tiles, most, LANES),
-            scratch(width + 2 * HALO + 8, LANES),
-            scratch(width + 2 * HALO + 8, LANES),
-            scratch(width + 2 * BORDER, LANES),
-            scratch(width + 2 * BORDER, LANES),
+            *[scratch(SLOTS, width + 2 * HALO + 8, LANES)] * 4,
+            *[scratch(SLOTS, width + 2 * BORDER, LANES)] * 2,
             scratch(2 * (tiles - 2), most + 2 * BORDER, LANES),
         ],
         20,
         80_000_000,
-        "early",
     )(x, by_core, by_y)
+    strip, pairs = ((2, deep + 8, LANES), f32), ((4, deep + 8, LANES), f32)
+    scanning = [scratch(8, LANES + 16, LANES), scratch(8, LANES + 8, LANES)]
+    *early, u1, u2, u3 = early
+    parts = [
+        ((width + LANES, width // 2 + width // 4 + LANES), bf16),
+        ((rows // 2, width // 2), f32),
+        ((rows // 4, width // 4), f32),
+        ((rows // 8, LANES), f32),
+    ]
+    middle = call(middle_kernel, [VMEM] * 10, [strip, pairs, *parts], scanning, 8, 10_000_000)(
+        a_ends, b_ends, corner_core, corner_y, u1, u2, u3, tents(width, False, False), at_left, at_right
+    )
     *outs, third = call(
         late_kernel,
-        [VMEM] * 17,
-        [((rows >> k, width >> k), f32) for k in range(3)] + [((width // 8, rows // 8), f32)],
-        [
-            scratch(2, deep + 8, LANES),
-            scratch(4, deep + 8, LANES),
-            scratch(4, LANES + 16, LANES),
-            scratch(4, LANES + 8, LANES),
+        [VMEM] * 13,
+        [strip, pairs] + [((rows >> k, width >> k), f32) for k in range(3)] + [((width // 8, rows // 8), f32)],
+        scanning
+        + [
             scratch(deep + 8, LANES),
             scratch(deep + 8, LANES),
             scratch(4, tall, LANES),
@@ -525,9 +602,10 @@
         ],
         20,
         80_000_000,
-        "late",
-    )(a_ends, b_ends, a_mid, b_mid, corner_core, corner_y, *early)
-    return (*outs, third.T)
+        [VMEM] * 2 + [ANY] * 4,
+        {2: 0, 3: 1},
+    )(a_mid, b_mid, *middle, *early)
+    return (*outs[2:], third.T)
 
 
 def solution(mesh):

time: 45.3 us -> 41.9 us (0.925)
  Pallas kernels: 20 us -> 16.5 us
    pallas_call x1, Pallas kernels: 10.6 us -> 8.31 us  [on_device(): call(early_kernel, [VMEM] * 3, [((3, most, LANES), f32), ((3, most, LANES...]
    pallas_call x2 -> x3, Pallas kernels: 9.09 us -> 7.94 us  [the longest x1 6.6 us: on_device(): call(late_kernel, [VMEM] * 13, [strip, pairs] + [((rows >> k, width >> k)...]
    unnamed x4 -> x10, local copies, waits for them, and re-layouts: 1.59 us -> 1.61 us
  transfers between devices with their start and end apart: 8 -> 8, of which waited for: 1 -> 1; matrix products, arithmetic and copies ran while one was open for 0% -> 0% of each run, Pallas kernels for 24% -> 23%
where the time goes in v1:
time: 41.9 us; the launch traced here: 41.7 us
  starting transfers between devices  16.6 us (40%)
  Pallas kernels  16.5 us (39%)
  waiting for transfers between devices  6.24 us (15%)
  local copies, waits for them, and re-layouts  1.61 us (4%)
  between operations  0.8 us (2%)
    ppermute x8, starting transfers between devices, swap(): return lax.ppermute(value, axis, pairs + [(j, i) for i, j in pairs])  16.6 us
    pallas_call x1, Pallas kernels, on_device(): call(early_kernel, [VMEM] * 3, [((3, most, LANES), f32), ((3, most, LANES...  8.31 us
    pallas_call x1, Pallas kernels, on_device(): call(late_kernel, [VMEM] * 13, [strip, pairs] + [((rows >> k, width >> k)...  6.6 us
    ppermute x8, waiting for transfers between devices, swap(): return lax.ppermute(value, axis, pairs + [(j, i) for i, j in pairs])  6.24 us
    unnamed x10, local copies, waits for them, and re-layouts  1.61 us
    pallas_call x1, Pallas kernels, on_device(): call(middle_kernel, [VMEM] * 10, [strip, pairs, *parts], scanning, 8, 100...  1.32 us
  transfers between devices with their start and end apart: 8, of which 1 were waited for; matrix products, arithmetic and copies ran while one was open for 0% of the time, Pallas kernels for 23%

profile of v1, /device:TPU:19, one launch (start us, length us, event | category | flops | bytes accessed | tf_op | source)
XLA Modules:
  0.0 41.7 jit_solution(17536435028435621562)
XLA Ops:
  0.6 0.0 copy-start
  0.6 1.6 %copy-done = f32[1024,512]{1,0:T(8,128)S(1)} copy-done((f32[1024,512]{1,0:T(8,128)S(1)}, f32[1024,512]{1,0:T(8,128)}, u32[]{:S(2)}) %copy-start) | copy-done | bytes 2097176
  2.2 0.0 copy-start.1
  2.2 0.3 shard_map.129
  2.5 0.0 copy-start.2
  2.5 0.0 copy-start.3
  2.5 0.0 copy-start.4
  2.5 0.3 collective-permute-start.2
  2.9 1.0 %collective-permute-start.6 = (f32[128,512]{1,0:T(8,128)S(1)}, f32[128,512]{1,0:T(8,128)S(1)}, u32[]{:S(2)}, u32[]{:S(2)}) collective-permute-start(f32[128,512]{1,0:T(8,128)S(1)} %get-tuple-element.36), channel_id=1, source_target_pairs={{0,8},{16,24},{8,0},{24,16},{1,9},{17,25},{9,1},{25,17},{2,10},{18... | collective-permute-start | bytes 786440 | tf_op jit(solution)/shard_map/ppermute | solution.py:532
  3.8 1.2 %collective-permute-start = (f32[768,128]{1,0:T(8,128)S(1)}, f32[768,128]{1,0:T(8,128)S(1)}, u32[]{:S(2)}, u32[]{:S(2)}) collective-permute-start(f32[768,128]{1,0:T(8,128)S(1)} %get-tuple-element.30), channel_id=1, source_target_pairs={{0,1},{2,3},{4,5},{6,7},{1,0},{3,2},{5,4},{7,6},{8,9},{10,11},{12,... | collective-permute-start | bytes 1179656 | tf_op jit(solution)/shard_map/ppermute | solution.py:532
  5.0 3.2 %collective-permute-start.1 = (f32[768,128]{1,0:T(8,128)S(1)}, f32[768,128]{1,0:T(8,128)S(1)}, u32[]{:S(2)}, u32[]{:S(2)}) collective-permute-start(f32[768,128]{1,0:T(8,128)S(1)} %get-tuple-element.31), channel_id=1, source_target_pairs={{1,2},{3,4},{5,6},{2,1},{4,3},{6,5},{9,10},{11,12},{13,14},{10,9},... | collective-permute-start | bytes 1179656 | tf_op jit(solution)/shard_map/ppermute | solution.py:532
  8.2 3.6 %collective-permute-start.7 = (f32[128,512]{1,0:T(8,128)S(1)}, f32[128,512]{1,0:T(8,128)S(1)}, u32[]{:S(2)}, u32[]{:S(2)}) collective-permute-start(f32[128,512]{1,0:T(8,128)S(1)} %get-tuple-element.37), channel_id=1, source_target_pairs={{8,16},{16,8},{9,17},{17,9},{10,18},{18,10},{11,19},{19,11},{12,20... | collective-permute-start | bytes 786440 | tf_op jit(solution)/shard_map/ppermute | solution.py:532
  11.8 0.0 collective-permute-done.2.a_ends
  11.8 3.0 %collective-permute-start.3 = (f32[256,128]{1,0:T(8,128)S(1)}, f32[256,128]{1,0:T(8,128)S(1)}, u32[]{:S(2)}, u32[]{:S(2)}) collective-permute-start(f32[256,128]{1,0:T(8,128)S(1)} %get-tuple-element.33), channel_id=1, source_target_pairs={{1,2},{3,4},{5,6},{2,1},{4,3},{6,5},{9,10},{11,12},{13,14},{10,9},... | collective-permute-start | bytes 393224 | tf_op jit(solution)/shard_map/ppermute | solution.py:532
  14.8 6.2 %collective-permute-done.3.b_ends = f32[256,128]{1,0:T(8,128)S(1)} collective-permute-done((f32[256,128]{1,0:T(8,128)S(1)}, f32[256,128]{1,0:T(8,128)S(1)}, u32[]{:S(2)}, u32[]{:S(2)}) %collective-permute-start.3) | collective-permute-done | bytes 131104 | tf_op jit(solution)/shard_map/ppermute | solution.py:532
  21.1 1.3 %collective-permute-start.4 = (f32[128,256]{1,0:T(8,128)S(1)}, f32[128,256]{1,0:T(8,128)S(1)}, u32[]{:S(2)}, u32[]{:S(2)}) collective-permute-start(f32[128,256]{1,0:T(8,128)S(1)} %get-tuple-element.34), channel_id=1, source_target_pairs={{0,8},{16,24},{8,0},{24,16},{1,9},{17,25},{9,1},{25,17},{2,10},{18... | collective-permute-start | bytes 393224 | tf_op jit(solution)/shard_map/ppermute | solution.py:532
  22.3 0.0 collective-permute-done.6.by_core
  22.3 3.1 %collective-permute-start.5 = (f32[128,256]{1,0:T(8,128)S(1)}, f32[128,256]{1,0:T(8,128)S(1)}, u32[]{:S(2)}, u32[]{:S(2)}) collective-permute-start(f32[128,256]{1,0:T(8,128)S(1)} %get-tuple-element.35), channel_id=1, source_target_pairs={{8,16},{16,8},{9,17},{17,9},{10,18},{18,10},{11,19},{19,11},{12,20... | collective-permute-start | bytes 393224 | tf_op jit(solution)/shard_map/ppermute | solution.py:532
  25.4 0.0 collective-permute-done.7.by_y
  25.4 0.0 copy-done.1
  25.4 8.3 %shard_map.131 = (f32[3,1152,128]{2,1,0:T(8,128)S(1)}, f32[3,1152,128]{2,1,0:T(8,128)S(1)}, f32[2,1152,128]{2,1,0:T(8,128)S(1)}, f32[1152,128]{1,0:T(8,128)S(1)}...) custom-call(f32[1024,512]{1,0:T(8,128)S(1)} %copy-done.1, ...), custom_call_target="tpu_custom_call" | custom-call | flops 80000000 | bytes 8000000 | tf_op jit(solution)/shard_map/pallas_call | solution.py:552
  33.7 0.0 collective-permute-done.4.by_core
  33.7 0.0 collective-permute-done.5.by_y
  33.8 0.0 copy-done.2
  33.8 0.0 copy-done.3
  33.8 0.0 copy-done.4
  33.8 1.3 %shard_map.132 = (f32[2,1288,128]{2,1,0:T(8,128)S(1)}, f32[4,1288,128]{2,1,0:T(8,128)S(1)}, bf16[640,512]{1,0:T(8,128)(2,1)S(1)}, f32[512,256]{1,0:T(8,128)S(1)}...) custom-call(f32[256,128]{1,0:T(8,128)S(1)} %collective-permute-done.2.a_ends, ...), custom_call_target="tpu_custom_call" | custom-call | flops 10000000 | bytes 8000000 | tf_op jit(solution)/shard_map/pallas_call | solution.py:584
  35.1 0.0 collective-permute-done.a_mid
  35.1 0.0 collective-permute-done.1.b_mid
  35.1 6.6 %shard_map.133 = (f32[2,1288,128]{2,1,0:T(8,128)S(1)}, f32[4,1288,128]{2,1,0:T(8,128)S(1)}, f32[1024,512]{1,0:T(8,128)}, f32[512,256]{1,0:T(8,128)}, f32[256,128]{1,0:T(8,128)}, /*index=5*/f32[64,128]{1,0:T(8,128)}) custom-call(f32[768,128]{1,0:T(8,128)S(1)} %collective-permute-done.a_mid, ...), custom_call_target="tpu_custom_call", output_to_operand_aliasing={{0}: (2, {}), {1}: (3, {})} | custom-call | flops 80000000 | bytes 8000000 | tf_op jit(solution)/shard_map/pallas_call | solution.py:587
  (1 shorter events, 0.0 us)
Async XLA Ops:
  0.6 1.6 %copy-start = (f32[1024,512]{1,0:T(8,128)S(1)}, f32[1024,512]{1,0:T(8,128)}, u32[]{:S(2)}) copy-start(f32[1024,512]{1,0:T(8,128)} %x.3) | copy-start | bytes 6291460
  2.2 23.2 %copy-start.1 = (f32[1024,512]{1,0:T(8,128)S(1)}, f32[1024,512]{1,0:T(8,128)}, u32[]{:S(2)}) copy-start(f32[1024,512]{1,0:T(8,128)} %x.3) | copy-start | bytes 6291460
  2.5 31.3 %copy-start.2 = (bf16[640,512]{1,0:T(8,128)(2,1)S(1)}, bf16[640,512]{1,0:T(8,128)(2,1)}, u32[]{:S(2)}) copy-start(bf16[640,512]{1,0:T(8,128)(2,1)} %constant.27.weights) | copy-start | bytes 1966084
  2.5 31.3 %copy-start.3 = (bf16[32,512]{1,0:T(8,128)(2,1)S(1)}, bf16[32,512]{1,0:T(8,128)(2,1)}, u32[]{:S(2)}) copy-start(bf16[32,512]{1,0:T(8,128)(2,1)} %constant.33.weights_right) | copy-start | bytes 98308
  2.5 31.3 %copy-start.4 = (bf16[32,512]{1,0:T(8,128)(2,1)S(1)}, bf16[32,512]{1,0:T(8,128)(2,1)}, u32[]{:S(2)}) copy-start(bf16[32,512]{1,0:T(8,128)(2,1)} %constant.31.weights_left) | copy-start | bytes 98308
  2.5 9.3 %collective-permute-start.2 = (f32[256,128]{1,0:T(8,128)S(1)}, f32[256,128]{1,0:T(8,128)S(1)}, u32[]{:S(2)}, u32[]{:S(2)}) collective-permute-start(f32[256,128]{1,0:T(8,128)S(1)} %get-tuple-element.32), channel_id=1, source_target_pairs={{0,1},{2,3},{4,5},{6,7},{1,0},{3,2},{5,4},{7,6},{8,9},{10,11},{12,... | collective-permute-start | bytes 393224 | tf_op jit(solution)/shard_map/ppermute | solution.py:532
  2.9 19.5 %collective-permute-start.6 = (f32[128,512]{1,0:T(8,128)S(1)}, f32[128,512]{1,0:T(8,128)S(1)}, u32[]{:S(2)}, u32[]{:S(2)}) collective-permute-start(f32[128,512]{1,0:T(8,128)S(1)} %get-tuple-element.36), channel_id=1, source_target_pairs={{0,8},{16,24},{8,0},{24,16},{1,9},{17,25},{9,1},{25,17},{2,10},{18... | collective-permute-start | bytes 786440 | tf_op jit(solution)/shard_map/ppermute | solution.py:532
  3.8 31.3 %collective-permute-start = (f32[768,128]{1,0:T(8,128)S(1)}, f32[768,128]{1,0:T(8,128)S(1)}, u32[]{:S(2)}, u32[]{:S(2)}) collective-permute-start(f32[768,128]{1,0:T(8,128)S(1)} %get-tuple-element.30), channel_id=1, source_target_pairs={{0,1},{2,3},{4,5},{6,7},{1,0},{3,2},{5,4},{7,6},{8,9},{10,11},{12,... | collective-permute-start | bytes 1179656 | tf_op jit(solution)/shard_map/ppermute | solution.py:532
  5.0 30.1 %collective-permute-start.1 = (f32[768,128]{1,0:T(8,128)S(1)}, f32[768,128]{1,0:T(8,128)S(1)}, u32[]{:S(2)}, u32[]{:S(2)}) collective-permute-start(f32[768,128]{1,0:T(8,128)S(1)} %get-tuple-element.31), channel_id=1, source_target_pairs={{1,2},{3,4},{5,6},{2,1},{4,3},{6,5},{9,10},{11,12},{13,14},{10,9},... | collective-permute-start | bytes 1179656 | tf_op jit(solution)/shard_map/ppermute | solution.py:532
  8.2 17.2 %collective-permute-start.7 = (f32[128,512]{1,0:T(8,128)S(1)}, f32[128,512]{1,0:T(8,128)S(1)}, u32[]{:S(2)}, u32[]{:S(2)}) collective-permute-start(f32[128,512]{1,0:T(8,128)S(1)} %get-tuple-element.37), channel_id=1, source_target_pairs={{8,16},{16,8},{9,17},{17,9},{10,18},{18,10},{11,19},{19,11},{12,20... | collective-permute-start | bytes 786440 | tf_op jit(solution)/shard_map/ppermute | solution.py:532
  11.8 9.2 %collective-permute-start.3 = (f32[256,128]{1,0:T(8,128)S(1)}, f32[256,128]{1,0:T(8,128)S(1)}, u32[]{:S(2)}, u32[]{:S(2)}) collective-permute-start(f32[256,128]{1,0:T(8,128)S(1)} %get-tuple-element.33), channel_id=1, source_target_pairs={{1,2},{3,4},{5,6},{2,1},{4,3},{6,5},{9,10},{11,12},{13,14},{10,9},... | collective-permute-start | bytes 393224 | tf_op jit(solution)/shard_map/ppermute | solution.py:532
  21.1 12.7 %collective-permute-start.4 = (f32[128,256]{1,0:T(8,128)S(1)}, f32[128,256]{1,0:T(8,128)S(1)}, u32[]{:S(2)}, u32[]{:S(2)}) collective-permute-start(f32[128,256]{1,0:T(8,128)S(1)} %get-tuple-element.34), channel_id=1, source_target_pairs={{0,8},{16,24},{8,0},{24,16},{1,9},{17,25},{9,1},{25,17},{2,10},{18... | collective-permute-start | bytes 393224 | tf_op jit(solution)/shard_map/ppermute | solution.py:532
  22.3 11.4 %collective-permute-start.5 = (f32[128,256]{1,0:T(8,128)S(1)}, f32[128,256]{1,0:T(8,128)S(1)}, u32[]{:S(2)}, u32[]{:S(2)}) collective-permute-start(f32[128,256]{1,0:T(8,128)S(1)} %get-tuple-element.35), channel_id=1, source_target_pairs={{8,16},{16,8},{9,17},{17,9},{10,18},{18,10},{11,19},{19,11},{12,20... | collective-permute-start | bytes 393224 | tf_op jit(solution)/shard_map/ppermute | solution.py:532
